TPU v7x, 32 devices: a whole 2x2x4 slice. The times are simulated.
32 devices in a mesh: gx: 4 (over z), gy: 4 (over y, x), gz: 2 (over core).
Axes of the slice: x: 2, y: 2, z: 4, core: 2. Of those that a mesh axis runs over, the one named last changes fastest.
Arguments:
- coefficients: bfloat16 [32, 64, 32, 128], P('gx', 'gy', 'gz'), may hold values from -0.109375 to 0.109375
- potential: float32 [32, 64, 32], P('gx', 'gy', 'gz'), may hold values from 0.5 to 2
- owner_map: int32 [4, 4, 2, 7, 1], P('gx', 'gy', 'gz'), may hold values from 0 to 3; in each aligned block of 7 rows (0 to 6, 7 to 13, ..., all dimensions but the last counted through in order) at most 2 rows name the same one
Outputs:
- correction: bfloat16 [4, 4, 2, 8, 128, 128], P('gx', 'gy', 'gz')
Inputs may be any that keep to these rules, and one draw needn't show every extreme that they name: `owner_map`: among the 7 blocks of one subdomain no owner is named more than 2 times; in every draw some subdomain names some owner exactly 2 times.
All inputs are finite; a program needn't handle non-finite values.
Results may differ from a plain program's by a relative error of at most 0.0062.
Values may be sent and summed in bfloat16 or wider, within the bound.
No kernel may reach another device: no remote copies, remote signals or barrier semaphores. Data moves between devices by JAX's collectives and lax.ppermute only.
A program may use at most 64 MiB of HBM per device.

v0:
```python
import math

import jax
import jax.numpy as jnp
from jax import lax
from jax.sharding import PartitionSpec as P

CAP = 2


SMOOTH = 0.25


def extended(cells, sides, width):
    for axis, dim in sides:
        count = lax.axis_size(axis)
        head = lax.slice_in_dim(cells, 0, width, axis=dim)
        tail = lax.slice_in_dim(cells, cells.shape[dim] - width, cells.shape[dim], axis=dim)
        cells = jnp.concatenate(
            [
                lax.ppermute(tail, axis, [(i, (i + 1) % count) for i in range(count)]),
                cells,
                lax.ppermute(head, axis, [((i + 1) % count, i) for i in range(count)]),
            ],
            axis=dim,
        )
    return cells


def moved(field, dim, step):
    count = field.shape[dim]
    zero = jnp.zeros_like(lax.slice_in_dim(field, 0, 1, axis=dim))
    if step > 0:
        return jnp.concatenate([lax.slice_in_dim(field, 1, count, axis=dim), zero], axis=dim)
    return jnp.concatenate([zero, lax.slice_in_dim(field, 0, count - 1, axis=dim)], axis=dim)


def neighbour_sum(field, dims):
    total = jnp.zeros(field.shape, jnp.float32)
    for dim in dims:
        total = (
            total
            + moved(field, dim, 1).astype(jnp.float32)
            + moved(field, dim, -1).astype(jnp.float32)
        )
    return total


def gram(left, right):
    width = left.shape[-1]
    return jnp.dot(
        left.reshape(-1, width).T,
        right.reshape(-1, right.shape[-1]),
        preferred_element_type=jnp.float32,
    )


def layer(field, dim, where):
    return lax.slice_in_dim(field, where, where + 1, axis=dim)


def local(coefficients, potential, owner_map):
    cells = coefficients.shape[:3]
    orbitals = coefficients.shape[3]
    smooth = (
        coefficients.astype(jnp.float32) + SMOOTH * neighbour_sum(coefficients, (0, 1, 2))
    ).astype(jnp.bfloat16)
    weighted = (potential[..., None] * smooth.astype(jnp.float32)).astype(jnp.bfloat16)
    hamilton = gram(smooth, weighted).astype(jnp.bfloat16)
    correlation = gram(smooth, smooth)
    faces = []
    padded = extended(coefficients, (("gx", 0), ("gy", 1), ("gz", 2)), 2)
    for dim in range(3):
        lateral = tuple((other for other in range(3) if other != dim))
        size = cells[dim]
        for side in (-1, 1):
            edge = 0 if side < 0 else size - 1
            c_own = layer(coefficients, dim, edge)
            s_own = layer(smooth, dim, edge)
            far_at = 1 if side < 0 else size + 2
            deep_at = 0 if side < 0 else size + 3
            slab = lax.slice_in_dim(
                padded, min(far_at, deep_at), min(far_at, deep_at) + 2, axis=dim
            )
            for other in lateral:
                slab = lax.slice_in_dim(slab, 2, 2 + cells[other], axis=other)
            far_local = far_at - min(far_at, deep_at)
            deep_local = deep_at - min(far_at, deep_at)
            c_far = layer(slab, dim, far_local)
            c_deep = layer(slab, dim, deep_local)
            s_far = (
                c_far.astype(jnp.float32)
                + SMOOTH * (c_deep.astype(jnp.float32) + neighbour_sum(c_far, lateral))
            ).astype(jnp.bfloat16)
            correlation = correlation + SMOOTH * SMOOTH * gram(c_own, c_own)
            faces.append(SMOOTH * (gram(s_own, c_far) + gram(c_own, s_far)))
    scale = jnp.float32(math.sqrt(cells[0] * cells[1] * cells[2]))
    blocks = jnp.stack([correlation - jnp.eye(orbitals, dtype=jnp.float32)] + faces)
    deviation = (scale * blocks).astype(jnp.bfloat16)
    count = deviation.shape[0]
    routes = owner_map.reshape(count)
    order = jnp.arange(count, dtype=jnp.int32)
    same = routes[:, None] == routes[None, :]
    earlier = order[None, :] < order[:, None]
    rank = jnp.sum((same & earlier).astype(jnp.int32), axis=1)
    owners = lax.axis_size("gx")
    target = (routes[None, None, :] == jnp.arange(owners, dtype=jnp.int32)[:, None, None]) & (
        rank[None, None, :] == jnp.arange(CAP, dtype=jnp.int32)[None, :, None]
    )
    pick = target.astype(jnp.bfloat16)
    product = jnp.einsum(
        "fab,bc->fac", deviation, hamilton, preferred_element_type=jnp.float32
    ).astype(jnp.bfloat16)
    chosen = jnp.einsum("osf,fab->osab", pick, product, preferred_element_type=jnp.float32).astype(
        jnp.bfloat16
    )
    result = lax.all_to_all(chosen, "gx", split_axis=0, concat_axis=0, tiled=True)
    return result.reshape(1, 1, 1, owners * CAP, orbitals, orbitals)


def solution(mesh):
    in_specs = (P("gx", "gy", "gz", None), P("gx", "gy", "gz"), P("gx", "gy", "gz", None, None))
    out_specs = P("gx", "gy", "gz", None, None, None)
    return jax.shard_map(local, mesh=mesh, in_specs=in_specs, out_specs=out_specs, check_vma=False)
```

profile of v0, /device:TPU:0, one launch (start us, length us, event | category | flops | bytes accessed | tf_op | source)
XLA Modules:
  0.0 37.8 jit_solution(1292740397561103388)
XLA Ops:
  0.0 1.0 %fusion.134 = (bf16[2,16,16,128]{3,2,1,0:T(8,128)(2,1)S(1)}, bf16[2,16,16,128]{3,2,1,0:T(8,128)(2,1)S(1)}) fusion(bf16[8,16,16,128]{3,2,1,0:T(8,128)(2,1)} %param.3), kind=kLoop, calls=%fused_computation.181 | loop fusion | bytes 524288 | tf_op jit(solution)/shard_map/slice | solution.py:17
  1.1 3.1 %collective-permute-start = (bf16[2,16,16,128]{3,1,2,0:T(8,128)(2,1)S(1)}, bf16[2,16,16,128]{3,1,2,0:T(8,128)(2,1)S(1)}, u32[]{:S(2)}, u32[]{:S(2)}) collective-permute-start(bf16[2,16,16,128]{3,1,2,0:T(8,128)(2,1)S(1)} %copy.183), channel_id=1, source_target_pairs={{0,8},{8,16},{16,24},{24,0},{1,9},{9,17},{17,25},{25,1},{2,10},{10... | collective-permute-start | bytes 393224 | tf_op jit(solution)/shard_map/ppermute | solution.py:21
  4.2 2.1 %collective-permute-start.1 = (bf16[2,16,16,128]{3,1,2,0:T(8,128)(2,1)S(1)}, bf16[2,16,16,128]{3,1,2,0:T(8,128)(2,1)S(1)}, u32[]{:S(2)}, u32[]{:S(2)}) collective-permute-start(bf16[2,16,16,128]{3,1,2,0:T(8,128)(2,1)S(1)} %copy.184), channel_id=1, source_target_pairs={{8,0},{16,8},{24,16},{0,24},{9,1},{17,9},{25,17},{1,25},{10,2},{18... | collective-permute-start | bytes 393224 | tf_op jit(solution)/shard_map/ppermute | solution.py:23
  6.3 0.2 fusion.138
  6.6 0.1 fusion.137
  6.7 0.2 fusion.136
  6.9 0.1 fusion.135
  7.0 0.6 %add_convert_fusion = bf16[8,16,16,128]{3,2,1,0:T(8,128)(2,1)S(1)} fusion(bf16[8,16,16,128]{3,2,1,0:T(8,128)(2,1)S(1)} %copy-done, bf16[8,16,15,128]{3,2,1,0:T(8,128)(2,1)S(1)} %get-tuple-element.22, bf16[8,16,15,128]{3,2,1,0:T(8,128)(2,1)S(1)} %get-tuple-element.21, bf16[8,15,16,128]{3,2,1,0:T(8,128)(2,1)S(1)} %get-tuple-element.20, ...), kind=kLoop, calls=%fused_computation.64 | loop fusion | flops 3932160 | bytes 3932160 | tf_op jit(solution)/shard_map/convert_element_type | solution.py:67
  7.7 0.3 convolution_bitcast_fusion.19
  8.1 0.6 %copy-done.2 = s32[1,1,1,7,1]{3,4,2,1,0:T(1,128)S(1)} copy-done((s32[1,1,1,7,1]{3,4,2,1,0:T(1,128)S(1)}, s32[1,1,1,7,1]{3,4,2,1,0:T(1,128)}, u32[]{:S(2)}) %copy-start.2) | copy-done | bytes 52
  8.8 0.2 convert_reduce_fusion
  9.0 0.2 fusion.14
  9.2 0.2 fusion.12
  9.4 0.2 fusion.10
  9.6 0.2 fusion.8
  9.8 0.2 fusion.6
  10.0 0.2 fusion.4
  10.2 0.4 %collective-permute-done = bf16[2,16,16,128]{3,1,2,0:T(8,128)(2,1)S(1)} collective-permute-done((bf16[2,16,16,128]{3,1,2,0:T(8,128)(2,1)S(1)}, bf16[2,16,16,128]{3,1,2,0:T(8,128)(2,1)S(1)}, u32[]{:S(2)}, u32[]{:S(2)}) %collective-permute-start) | collective-permute-done | bytes 131104 | tf_op jit(solution)/shard_map/ppermute | solution.py:21
  10.6 0.2 constant_dynamic-update-slice_fusion.1
  10.8 1.3 %collective-permute-done.1 = bf16[2,16,16,128]{3,1,2,0:T(8,128)(2,1)S(1)} collective-permute-done((bf16[2,16,16,128]{3,1,2,0:T(8,128)(2,1)S(1)}, bf16[2,16,16,128]{3,1,2,0:T(8,128)(2,1)S(1)}, u32[]{:S(2)}, u32[]{:S(2)}) %collective-permute-start.1) | collective-permute-done | bytes 131104 | tf_op jit(solution)/shard_map/ppermute | solution.py:23
  12.1 0.2 fusion.132
  12.2 1.5 %collective-permute-start.2 = (bf16[12,2,16,128]{3,1,2,0:T(2,128)(2,1)S(1)}, bf16[12,2,16,128]{3,1,2,0:T(2,128)(2,1)S(1)}, u32[]{:S(2)}, u32[]{:S(2)}) collective-permute-start(bf16[12,2,16,128]{3,1,2,0:T(2,128)(2,1)S(1)} %get-tuple-element.8), channel_id=1, source_target_pairs={{0,2},{2,4},{4,6},{6,0},{1,3},{3,5},{5,7},{7,1},{8,10},{10,12},{12... | collective-permute-start | bytes 294920 | tf_op jit(solution)/shard_map/ppermute | solution.py:21
  13.8 1.4 %collective-permute-start.3 = (bf16[12,2,16,128]{3,1,2,0:T(2,128)(2,1)S(1)}, bf16[12,2,16,128]{3,1,2,0:T(2,128)(2,1)S(1)}, u32[]{:S(2)}, u32[]{:S(2)}) collective-permute-start(bf16[12,2,16,128]{3,1,2,0:T(2,128)(2,1)S(1)} %get-tuple-element.7), channel_id=1, source_target_pairs={{2,0},{4,2},{6,4},{0,6},{3,1},{5,3},{7,5},{1,7},{10,8},{12,10},{14... | collective-permute-start | bytes 294920 | tf_op jit(solution)/shard_map/ppermute | solution.py:23
  15.3 0.2 convolution_bitcast_fusion.11
  15.5 0.2 fusion.18
  15.8 0.2 convolution_bitcast_fusion.9
  16.0 0.2 fusion.22
  16.2 2.5 %collective-permute-done.2 = bf16[12,2,16,128]{3,1,2,0:T(2,128)(2,1)S(1)} collective-permute-done((bf16[12,2,16,128]{3,1,2,0:T(2,128)(2,1)S(1)}, bf16[12,2,16,128]{3,1,2,0:T(2,128)(2,1)S(1)}, u32[]{:S(2)}, u32[]{:S(2)}) %collective-permute-start.2) | collective-permute-done | bytes 98336 | tf_op jit(solution)/shard_map/ppermute | solution.py:21
  18.9 0.3 fusion.72
  19.2 0.2 convolution_bitcast_fusion.7
  19.4 0.2 collective-permute-done.3
  19.7 0.3 fusion.73
  20.0 0.2 convolution_bitcast_fusion.5
  20.2 0.2 pad_maximum_fusion
  20.5 0.5 %collective-permute-start.5 = (bf16[12,20,2,128]{3,1,2,0:T(8,128)(2,1)S(1)}, bf16[12,20,2,128]{3,1,2,0:T(8,128)(2,1)S(1)}, u32[]{:S(2)}, u32[]{:S(2)}) collective-permute-start(bf16[12,20,2,128]{3,1,2,0:T(8,128)(2,1)S(1)} %get-tuple-element.5), channel_id=1, source_target_pairs={{1,0},{0,1},{3,2},{2,3},{5,4},{4,5},{7,6},{6,7},{9,8},{8,9},{11,10... | collective-permute-start | bytes 368648 | tf_op jit(solution)/shard_map/ppermute | solution.py:23
  21.1 0.2 fusion.26
  21.3 0.2 fusion.30
  21.5 0.3 collective-permute-done.4
  21.9 0.2 collective-permute-done.5
  22.1 0.2 convolution_bitcast_fusion.3
  22.3 0.2 fusion.34
  22.5 0.2 convolution_bitcast_fusion.1
  22.7 0.2 fusion.38
  22.9 0.6 %copy-done.1 = f32[8,16,16]{2,1,0:T(8,128)S(1)} copy-done((f32[8,16,16]{2,1,0:T(8,128)S(1)}, f32[8,16,16]{2,1,0:T(8,128)}, u32[]{:S(2)}) %copy-start.1) | copy-done | bytes 8216
  23.6 0.8 %convolution_convert_fusion.1 = bf16[7,128,128]{2,1,0:T(8,128)(2,1)S(1)} fusion(bf16[8,16,16,128]{3,2,1,0:T(8,128)(2,1)S(1)} %add_convert_fusion, f32[8,16,16]{2,1,0:T(8,128)S(1)} %copy-done.1, f32[7,128,128]{2,1,0:T(8,128)S(1)} %fusion.38), kind=kOutput, calls=%fused_computation.1 | convolution fusion | flops 97615872 | bytes 1220608 | tf_op jit(solution)/shard_map/fab,bc->fac/dot_general | solution.py:111
  24.4 0.3 convolution_convert_fusion
  24.7 12.3 %all_to_all.5 = bf16[4,2,128,128]{3,2,1,0:T(8,128)(2,1)S(1)} all-to-all(bf16[4,2,128,128]{3,2,1,0:T(8,128)(2,1)S(1)} %copy.114), channel_id=1, replica_groups=mesh['gx'=4,'gy'=4,'gz'=2] {'gx'}, dimensions={0} | all-to-all | bytes 524288 | tf_op jit(solution)/shard_map/all_to_all | solution.py:117
  37.1 0.7 %copy.194 = bf16[1,1,1,8,128,128]{5,4,3,2,1,0:T(8,128)(2,1)} copy(bf16[1,1,1,8,128,128]{5,4,3,2,1,0:T(8,128)(2,1)S(1)} %bitcast.265) | data formatting | bytes 524288
  (30 shorter events, 0.9 us)
Async XLA Ops:
  0.0 6.3 %copy-start = (bf16[8,16,16,128]{3,2,1,0:T(8,128)(2,1)S(1)}, bf16[8,16,16,128]{3,2,1,0:T(8,128)(2,1)}, u32[]{:S(2)}) copy-start(bf16[8,16,16,128]{3,2,1,0:T(8,128)(2,1)} %param.3) | copy-start | bytes 1572868
  1.1 9.5 %collective-permute-start = (bf16[2,16,16,128]{3,1,2,0:T(8,128)(2,1)S(1)}, bf16[2,16,16,128]{3,1,2,0:T(8,128)(2,1)S(1)}, u32[]{:S(2)}, u32[]{:S(2)}) collective-permute-start(bf16[2,16,16,128]{3,1,2,0:T(8,128)(2,1)S(1)} %copy.183), channel_id=1, source_target_pairs={{0,8},{8,16},{16,24},{24,0},{1,9},{9,17},{17,25},{25,1},{2,10},{10... | collective-permute-start | bytes 393224 | tf_op jit(solution)/shard_map/ppermute | solution.py:21
  4.2 7.8 %collective-permute-start.1 = (bf16[2,16,16,128]{3,1,2,0:T(8,128)(2,1)S(1)}, bf16[2,16,16,128]{3,1,2,0:T(8,128)(2,1)S(1)}, u32[]{:S(2)}, u32[]{:S(2)}) collective-permute-start(bf16[2,16,16,128]{3,1,2,0:T(8,128)(2,1)S(1)} %copy.184), channel_id=1, source_target_pairs={{8,0},{16,8},{24,16},{0,24},{9,1},{17,9},{25,17},{1,25},{10,2},{18... | collective-permute-start | bytes 393224 | tf_op jit(solution)/shard_map/ppermute | solution.py:23
  8.1 0.7 %copy-start.2 = (s32[1,1,1,7,1]{3,4,2,1,0:T(1,128)S(1)}, s32[1,1,1,7,1]{3,4,2,1,0:T(1,128)}, u32[]{:S(2)}) copy-start(s32[1,1,1,7,1]{3,4,2,1,0:T(1,128)} %param.5) | copy-start | bytes 88
  12.2 6.5 %collective-permute-start.2 = (bf16[12,2,16,128]{3,1,2,0:T(2,128)(2,1)S(1)}, bf16[12,2,16,128]{3,1,2,0:T(2,128)(2,1)S(1)}, u32[]{:S(2)}, u32[]{:S(2)}) collective-permute-start(bf16[12,2,16,128]{3,1,2,0:T(2,128)(2,1)S(1)} %get-tuple-element.8), channel_id=1, source_target_pairs={{0,2},{2,4},{4,6},{6,0},{1,3},{3,5},{5,7},{7,1},{8,10},{10,12},{12... | collective-permute-start | bytes 294920 | tf_op jit(solution)/shard_map/ppermute | solution.py:21
  13.8 5.8 %collective-permute-start.3 = (bf16[12,2,16,128]{3,1,2,0:T(2,128)(2,1)S(1)}, bf16[12,2,16,128]{3,1,2,0:T(2,128)(2,1)S(1)}, u32[]{:S(2)}, u32[]{:S(2)}) collective-permute-start(bf16[12,2,16,128]{3,1,2,0:T(2,128)(2,1)S(1)} %get-tuple-element.7), channel_id=1, source_target_pairs={{2,0},{4,2},{6,4},{0,6},{3,1},{5,3},{7,5},{1,7},{10,8},{12,10},{14... | collective-permute-start | bytes 294920 | tf_op jit(solution)/shard_map/ppermute | solution.py:23
  20.4 1.4 %collective-permute-start.4 = (bf16[12,20,2,128]{3,1,2,0:T(8,128)(2,1)S(1)}, bf16[12,20,2,128]{3,1,2,0:T(8,128)(2,1)S(1)}, u32[]{:S(2)}, u32[]{:S(2)}) collective-permute-start(bf16[12,20,2,128]{3,1,2,0:T(8,128)(2,1)S(1)} %get-tuple-element.6), channel_id=1, source_target_pairs={{0,1},{1,0},{2,3},{3,2},{4,5},{5,4},{6,7},{7,6},{8,9},{9,8},{10,11... | collective-permute-start | bytes 368648 | tf_op jit(solution)/shard_map/ppermute | solution.py:21
  20.5 1.6 %collective-permute-start.5 = (bf16[12,20,2,128]{3,1,2,0:T(8,128)(2,1)S(1)}, bf16[12,20,2,128]{3,1,2,0:T(8,128)(2,1)S(1)}, u32[]{:S(2)}, u32[]{:S(2)}) collective-permute-start(bf16[12,20,2,128]{3,1,2,0:T(8,128)(2,1)S(1)} %get-tuple-element.5), channel_id=1, source_target_pairs={{1,0},{0,1},{3,2},{2,3},{5,4},{4,5},{7,6},{6,7},{9,8},{8,9},{11,10... | collective-permute-start | bytes 368648 | tf_op jit(solution)/shard_map/ppermute | solution.py:23
  22.7 0.8 %copy-start.1 = (f32[8,16,16]{2,1,0:T(8,128)S(1)}, f32[8,16,16]{2,1,0:T(8,128)}, u32[]{:S(2)}) copy-start(f32[8,16,16]{2,1,0:T(8,128)} %param.4) | copy-start | bytes 24580
where the time goes:
time: 38 us; the launch traced here: 37.8 us
  blocking collectives  12.3 us (32%)
  starting transfers between devices  8.75 us (23%)
  matrix products  5.04 us (13%)
  waiting for transfers between devices  4.88 us (13%)
  local copies, waits for them, and re-layouts  4.87 us (13%)
  other arithmetic  1.58 us (4%)
    all_to_all x1, blocking collectives, local(): lax.all_to_all(chosen, 'gx', split_axis=0, concat_axis=0, tiled=True)  12.3 us
    ppermute x3, starting transfers between devices, extended(): lax.ppermute(tail, axis, [(i, (i + 1) % count) for i in range(count)])  4.72 us
    ppermute x3, starting transfers between devices, extended(): lax.ppermute(head, axis, [((i + 1) % count, i) for i in range(count)])  4.03 us
    dot_general x19, matrix products, gram(): jnp.dot(left.reshape(-1, width).T, right.reshape(-1, right.shape[-1]), pr...  3.95 us
    ppermute x3, waiting for transfers between devices, extended(): lax.ppermute(tail, axis, [(i, (i + 1) % count) for i in range(count)])  3.23 us
    unnamed x11, local copies, waits for them, and re-layouts  2.25 us
    ppermute x3, waiting for transfers between devices, extended(): lax.ppermute(head, axis, [((i + 1) % count, i) for i in range(count)])  1.65 us
    slice x2, local copies, waits for them, and re-layouts, extended(): head = lax.slice_in_dim(cells, 0, width, axis=dim)  1.2 us
  transfers between devices with their start and end apart: 6, of which 6 were waited for; matrix products, arithmetic and copies ran while one was open for 14% of the time, Pallas kernels for 0%

commit v1 on v0

v1 whole, which is shorter than its diff:
```python
import functools
import math

import jax
import jax.numpy as jnp
from jax import lax
from jax.experimental import pallas as pl
from jax.experimental.pallas import tpu as pltpu
from jax.sharding import PartitionSpec as P


CAP = 2
SMOOTH = 0.25
F32 = jnp.float32
BF16 = jnp.bfloat16


def halo(low, high, axis):
    count = lax.axis_size(axis)
    up = [(i, (i + 1) % count) for i in range(count)]
    down = [((i + 1) % count, i) for i in range(count)]
    if count == 2:
        both = lax.ppermute(jnp.concatenate([high, low], axis=0), axis, up)
        return both[: high.shape[0]], both[high.shape[0] :]
    from_low = lax.ppermute(high, axis, up)
    return from_low, lax.ppermute(low, axis, down)


def local_kernel(cells, owners, c_ref, v_ref, route_ref, me_ref, lt_ref, dev_ref, ham_ref, slot_ref, c32, s32, sb, lz, lc):
    cx, cy, cz = cells
    plane = cy * cz
    width = c_ref.shape[1]
    rows = lax.broadcasted_iota(jnp.int32, (plane, plane), 0)
    cols = lax.broadcasted_iota(jnp.int32, (plane, plane), 1)
    gap = jnp.abs(rows - cols)
    beside = (gap == cz) | ((gap == 1) & ((rows // cz) == (cols // cz)))
    lateral = jnp.where(gap == 0, 1.0, jnp.where(beside, SMOOTH, 0.0)).astype(BF16)

    for x in range(cx):
        here = c_ref[x * plane : (x + 1) * plane, :]
        c32[x * plane : (x + 1) * plane, :] = here.astype(F32)
    for x in range(cx):
        at = slice(x * plane, (x + 1) * plane)
        total = jnp.dot(lateral, c_ref[at, :], preferred_element_type=F32)
        beyond = [c32[(x + d) * plane : (x + d + 1) * plane, :] for d in (-1, 1) if 0 <= x + d < cx]
        for other in beyond:
            total = total + SMOOTH * other
        s32[at, :] = total
        sb[at, :] = total.astype(BF16)

    lc[...] = jnp.zeros_like(lc)
    offset = 0
    for side in (0, 1):
        edge, deep = (0, 1) if side == 0 else (cx - 1, cx - 2)
        p = 2.0 * s32[edge * plane : (edge + 1) * plane, :] - SMOOTH * c32[deep * plane : (deep + 1) * plane, :]
        q = SMOOTH * c32[edge * plane : (edge + 1) * plane, :]
        q = q.astype(BF16)
        p = p.astype(BF16)
        first, second = (q, p) if side == 0 else (p, q)
        lt_ref[:, offset : offset + plane] = first.T
        lt_ref[:, offset + plane : offset + 2 * plane] = second.T
        shift = offset if side == 0 else offset + plane
        lc[shift : shift + plane, :] = q
        offset += 2 * plane
    for side in (0, 1):
        edge, deep = (0, 1) if side == 0 else (cy - 1, cy - 2)
        pieces = []
        for x in range(cx):
            a = x * plane + edge * cz
            b = x * plane + deep * cz
            p = (2.0 * s32[a : a + cz, :] - SMOOTH * c32[b : b + cz, :]).astype(BF16)
            q = (SMOOTH * c32[a : a + cz, :]).astype(BF16)
            pieces += [q, p] if side == 0 else [p, q]
            shift = offset + 2 * x * cz + (0 if side == 0 else cz)
            lc[shift : shift + cz, :] = q
        stacked = jnp.concatenate(pieces, axis=0)
        lt_ref[:, offset : offset + 2 * cx * cz] = stacked.T
        offset += 2 * cx * cz
    area = cx * cy
    for side in (0, 1):
        edge, deep = (0, 1) if side == 0 else (cz - 1, cz - 2)
        q = SMOOTH * c32[pl.ds(edge, area, stride=cz), :]
        p = 2.0 * s32[pl.ds(edge, area, stride=cz), :] - SMOOTH * c32[pl.ds(deep, area, stride=cz), :]
        lz[pl.ds(0 if side == 0 else 1, area, stride=2), :] = q
        lz[pl.ds(1 if side == 0 else 0, area, stride=2), :] = jnp.zeros_like(q)
        lc[offset : offset + 2 * area, :] = lz[...].astype(BF16)
        lz[pl.ds(1 if side == 0 else 0, area, stride=2), :] = p
        lt_ref[:, offset : offset + 2 * area] = lz[...].astype(BF16).T
        offset += 2 * area

    gram = jnp.dot(lt_ref[...], lc[...], preferred_element_type=F32)
    ham = jnp.zeros((width, width), F32)
    for x in range(cx):
        at = slice(x * plane, (x + 1) * plane)
        turned = sb[at, :].T
        weighted = (turned.astype(F32) * v_ref[:, at]).astype(BF16)
        both = jnp.dot(jnp.concatenate([turned, weighted], axis=0), sb[at, :], preferred_element_type=F32)
        gram = gram + both[:width]
        ham = ham + both[width:]
    ham_ref[...] = ham.astype(BF16)
    eye = (lax.broadcasted_iota(jnp.int32, (width, width), 0) == lax.broadcasted_iota(jnp.int32, (width, width), 1)).astype(F32)
    scale = math.sqrt(cx * cy * cz)
    dev_ref[...] = (scale * (gram - eye)).astype(BF16)

    count = slot_ref.shape[0]
    me = me_ref[0]
    for b in range(count):
        rank = jnp.int32(0)
        for a in range(b):
            rank = rank + (route_ref[a] == route_ref[b]).astype(jnp.int32)
        ahead = lax.rem(route_ref[b] - me + owners, owners)
        slot_ref[b, :, :] = jnp.full(slot_ref.shape[1:], ahead * CAP + rank, jnp.int32)


def place(slot_ref, b, slot, block, old):
    return jnp.where(slot_ref[b, :1, :] == slot, block, old)


def early_kernel(scale, offsets, slots, lt_ref, dev_ref, ham_ref, slot_ref, yl, yh, zl, zh, out_ref):
    ham = ham_ref[...]
    blocks = [dev_ref[...]]
    for offset, far in zip(offsets, (yl, yh, zl, zh)):
        face = jnp.dot(lt_ref[:, offset : offset + far.shape[0]], far[...], preferred_element_type=F32)
        blocks.append((scale * face).astype(BF16))
    width = ham.shape[0]
    product = jnp.dot(jnp.concatenate(blocks, axis=0), ham, preferred_element_type=F32)
    for slot in range(slots):
        total = jnp.zeros((width, width), F32)
        for i, b in enumerate((0, 3, 4, 5, 6)):
            total = place(slot_ref, b, slot, product[i * width : (i + 1) * width], total)
        out_ref[slot, :, :] = total.astype(BF16)


def late_kernel(scale, lt_ref, ham_ref, slot_ref, xl, xh, early_ref, out_ref):
    ham = ham_ref[...]
    width = ham.shape[0]
    blocks = []
    offset = 0
    for far in (xl, xh):
        face = jnp.dot(lt_ref[:, offset : offset + far.shape[0]], far[...], preferred_element_type=F32)
        blocks.append((scale * face).astype(BF16))
        offset += far.shape[0]
    product = jnp.dot(jnp.concatenate(blocks, axis=0), ham, preferred_element_type=F32)
    for slot in range(out_ref.shape[0]):
        total = early_ref[slot, :, :].astype(F32)
        for i, b in enumerate((1, 2)):
            total = place(slot_ref, b, slot, product[i * width : (i + 1) * width], total)
        out_ref[slot, :, :] = total.astype(BF16)


def local(coefficients, potential, owner_map):
    cells = coefficients.shape[:3]
    cx, cy, cz = cells
    width = coefficients.shape[3]
    blocks = owner_map.shape[3]
    owners = lax.axis_size("gx")
    me = lax.axis_index("gx")
    slots = owners * CAP
    total = cx * cy * cz
    flat = lambda layers: layers.reshape(-1, width)

    x_low, x_high = halo(flat(coefficients[:2]), flat(coefficients[cx - 2 :]), "gx")
    y_low, y_high = halo(flat(coefficients[:, :2]), flat(coefficients[:, cy - 2 :]), "gy")
    z_low, z_high = halo(flat(coefficients[:, :, :2]), flat(coefficients[:, :, cz - 2 :]), "gz")

    vmem = pl.BlockSpec(memory_space=pltpu.VMEM)
    smem = pl.BlockSpec(memory_space=pltpu.SMEM)
    factors = 4 * (cy * cz + cx * cz + cx * cy)
    sds = jax.ShapeDtypeStruct
    lt, dev, ham, slot = pl.pallas_call(
        functools.partial(local_kernel, cells, owners),
        name="own_cells",
        out_shape=(
            sds((width, factors), BF16),
            sds((width, width), BF16),
            sds((width, width), BF16),
            sds((blocks, 8, width), jnp.int32),
        ),
        in_specs=[vmem, vmem, smem, smem],
        out_specs=[vmem] * 4,
        scratch_shapes=[
            pltpu.VMEM((total, width), F32),
            pltpu.VMEM((total, width), F32),
            pltpu.VMEM((total, width), BF16),
            pltpu.VMEM((2 * cx * cy, width), F32),
            pltpu.VMEM((factors, width), BF16),
        ],
        compiler_params=pltpu.CompilerParams(vmem_limit_bytes=16 << 20),
        cost_estimate=pl.CostEstimate(flops=2_000_000_000, bytes_accessed=2 * total * width, transcendentals=0),
    )(flat(coefficients), potential.reshape(1, total), owner_map.reshape(blocks), me.reshape(1))

    scale = SMOOTH * math.sqrt(total)
    at_y = 4 * cy * cz
    at_z = at_y + 4 * cx * cz
    offsets = (at_y, at_y + 2 * cx * cz, at_z, at_z + 2 * cx * cy)
    early = pl.pallas_call(
        functools.partial(early_kernel, scale, offsets, slots),
        name="lateral_faces",
        out_shape=sds((slots, width, width), BF16),
        in_specs=[vmem] * 8,
        out_specs=vmem,
        compiler_params=pltpu.CompilerParams(vmem_limit_bytes=8 << 20),
        cost_estimate=pl.CostEstimate(flops=500_000_000, bytes_accessed=total * width, transcendentals=0),
    )(lt, dev, ham, slot, y_low, y_high, z_low, z_high)
    chosen = pl.pallas_call(
        functools.partial(late_kernel, scale),
        name="first_faces",
        out_shape=sds((slots, width, width), BF16),
        in_specs=[vmem] * 6,
        out_specs=vmem,
        compiler_params=pltpu.CompilerParams(vmem_limit_bytes=8 << 20),
        cost_estimate=pl.CostEstimate(flops=500_000_000, bytes_accessed=total * width, transcendentals=0),
    )(lt, ham, slot, x_low, x_high, early)

    pieces = [chosen[:CAP]]
    for step in range(1, owners):
        route = [(i, (i + step) % owners) for i in range(owners)]
        pieces.append(lax.ppermute(chosen[step * CAP : (step + 1) * CAP], "gx", route))

    def gather_kernel(me_ref, *refs):
        ins, out_ref, sems = refs[:owners], refs[owners], refs[owners + 1]
        copies = []
        for step in range(owners):
            source = lax.rem(me_ref[0] + owners - step, owners)
            copies.append(pltpu.make_async_copy(ins[step], out_ref.at[pl.ds(source * CAP, CAP)], sems.at[step]))
        for copy in copies:
            copy.start()
        for copy in copies:
            copy.wait()

    result = pl.pallas_call(
        gather_kernel,
        name="gather_slots",
        out_shape=sds((slots, width, width), BF16),
        in_specs=[smem] + [vmem] * owners,
        out_specs=pl.BlockSpec(memory_space=pl.ANY),
        scratch_shapes=[pltpu.SemaphoreType.DMA((owners,))],
        compiler_params=pltpu.CompilerParams(vmem_limit_bytes=8 << 20),
    )(me.reshape(1), *pieces)
    return result.reshape(1, 1, 1, slots, width, width)


def solution(mesh):
    in_specs = (P("gx", "gy", "gz", None), P("gx", "gy", "gz"), P("gx", "gy", "gz", None, None))
    out_specs = P("gx", "gy", "gz", None, None, None)
    return jax.shard_map(local, mesh=mesh, in_specs=in_specs, out_specs=out_specs, check_vma=False)
```

time: 38 us -> 24.8 us (0.65)
  blocking collectives: 12.3 us -> 0 us
  matrix products: 5.04 us -> 0 us
  starting transfers between devices: 8.75 us -> 12.5 us
  Pallas kernels: 0 us -> 3.28 us
  local copies, waits for them, and re-layouts: 4.87 us -> 2 us
  waiting for transfers between devices: 4.88 us -> 6.75 us
  other arithmetic: 1.58 us -> 0.01 us
    all_to_all x1 -> x0, blocking collectives: 12.3 us -> none  [local(): lax.all_to_all(chosen, 'gx', split_axis=0, concat_axis=0, tiled=True)]
    dot_general x21 -> x0, matrix products: 5.04 us -> none  [the longest x19 3.95 us: gram(): jnp.dot(left.reshape(-1, width).T, right.reshape(-1, right.shape[-1]), pr...]
    ppermute x6 -> x8, starting transfers between devices: 8.75 us -> 12.5 us  [the longest x2 4.58 us: halo(): from_low = lax.ppermute(high, axis, up)]
    pallas_call x0 -> x4, Pallas kernels: none -> 3.28 us  [the longest x1 1.76 us: local(): pl.pallas_call(functools.partial(local_kernel, cells, owners), name='own_...]
    ppermute x6 -> x8, waiting for transfers between devices: 4.88 us -> 6.75 us  [the longest x3 3.97 us: local(): lax.ppermute(chosen[step * CAP:(step + 1) * CAP], 'gx', route)]
    unnamed x11 -> x6, local copies, waits for them, and re-layouts: 2.25 us -> 0.66 us
    slice x21 -> x5, local copies, waits for them, and re-layouts: 2.54 us -> 1.25 us  [the longest x1 1.19 us: local(): coefficients[:, :, cz - 2:]]
    convert_element_type x3 -> x0, other arithmetic: 1.22 us -> none  [the longest x1 0.63 us: local(): smooth = (coefficients.astype(jnp.float32) + SMOOTH * neighbour_sum(coeff...]
  transfers between devices with their start and end apart: 6 -> 8, of which waited for: 6 -> 4; matrix products, arithmetic and copies ran while one was open for 14% -> 1% of each run, Pallas kernels for 0% -> 9%
where the time goes in v1:
time: 24.8 us; the launch traced here: 24.7 us
  starting transfers between devices  12.5 us (50%)
  waiting for transfers between devices  6.75 us (27%)
  Pallas kernels  3.28 us (13%)
  local copies, waits for them, and re-layouts  2 us (8%)
    ppermute x2, starting transfers between devices, halo(): from_low = lax.ppermute(high, axis, up)  4.58 us
    ppermute x3, starting transfers between devices, local(): lax.ppermute(chosen[step * CAP:(step + 1) * CAP], 'gx', route)  4.27 us
    ppermute x3, waiting for transfers between devices, local(): lax.ppermute(chosen[step * CAP:(step + 1) * CAP], 'gx', route)  3.97 us
    ppermute x2, starting transfers between devices, halo(): return (from_low, lax.ppermute(low, axis, down))  3.12 us
    pallas_call x1, Pallas kernels, local(): pl.pallas_call(functools.partial(local_kernel, cells, owners), name='own_...  1.76 us
    ppermute x2, waiting for transfers between devices, halo(): return (from_low, lax.ppermute(low, axis, down))  1.47 us
    ppermute x2, waiting for transfers between devices, halo(): from_low = lax.ppermute(high, axis, up)  1.31 us
    slice x1, local copies, waits for them, and re-layouts, local(): coefficients[:, :, cz - 2:]  1.19 us
  transfers between devices with their start and end apart: 8, of which 4 were waited for; matrix products, arithmetic and copies ran while one was open for 1% of the time, Pallas kernels for 9%

profile of v1, /device:TPU:0, one launch (start us, length us, event | category | flops | bytes accessed | tf_op | source)
XLA Modules:
  0.0 24.7 jit_solution(9940919470864444454)
XLA Ops:
  0.0 0.0 copy-start
  0.0 1.2 %fusion = (bf16[8,16,2,128]{3,2,1,0:T(2,128)(2,1)S(1)}, bf16[8,16,2,128]{3,2,1,0:T(2,128)(2,1)S(1)}) fusion(bf16[8,16,16,128]{3,2,1,0:T(8,128)(2,1)} %param.3), kind=kLoop, calls=%fused_computation.1 | loop fusion | bytes 262144 | tf_op jit(solution)/shard_map/slice | solution.py:164
  1.2 0.6 %collective-permute-start.4 = (bf16[512,128]{1,0:T(8,128)(2,1)S(1)}, bf16[512,128]{1,0:T(8,128)(2,1)S(1)}, u32[]{:S(2)}, u32[]{:S(2)}) collective-permute-start(bf16[512,128]{1,0:T(8,128)(2,1)S(1)} %pad_maximum_fusion), channel_id=1, source_target_pairs={{0,1},{1,0},{2,3},{3,2},{4,5},{5,4},{6,7},{7,6},{8,9},{9,8},{10,11... | collective-permute-start | bytes 393224 | tf_op jit(solution)/shard_map/ppermute | solution.py:23
  1.8 0.0 copy-done
  1.8 2.6 %collective-permute-start.2 = (bf16[256,128]{1,0:T(8,128)(2,1)S(1)}, bf16[256,128]{1,0:T(8,128)(2,1)S(1)}, u32[]{:S(2)}, u32[]{:S(2)}) collective-permute-start(bf16[256,128]{1,0:T(8,128)(2,1)S(1)} %bitcast.17), channel_id=1, source_target_pairs={{0,2},{2,4},{4,6},{6,0},{1,3},{3,5},{5,7},{7,1},{8,10},{10,12},{12... | collective-permute-start | bytes 196616 | tf_op jit(solution)/shard_map/ppermute | solution.py:25
  4.3 0.0 copy-start.2
  4.3 1.0 %collective-permute-start.3 = (bf16[256,128]{1,0:T(8,128)(2,1)S(1)}, bf16[256,128]{1,0:T(8,128)(2,1)S(1)}, u32[]{:S(2)}, u32[]{:S(2)}) collective-permute-start(bf16[256,128]{1,0:T(8,128)(2,1)S(1)} %bitcast.16), channel_id=1, source_target_pairs={{2,0},{4,2},{6,4},{0,6},{3,1},{5,3},{7,5},{1,7},{10,8},{12,10},{14... | collective-permute-start | bytes 196616 | tf_op jit(solution)/shard_map/ppermute | solution.py:26
  5.4 2.0 %collective-permute-start = (bf16[512,128]{1,0:T(8,128)(2,1)S(1)}, bf16[512,128]{1,0:T(8,128)(2,1)S(1)}, u32[]{:S(2)}, u32[]{:S(2)}) collective-permute-start(bf16[512,128]{1,0:T(8,128)(2,1)S(1)} %bitcast.15), channel_id=1, source_target_pairs={{0,8},{8,16},{16,24},{24,0},{1,9},{9,17},{17,25},{25,1},{2,10},{10... | collective-permute-start | bytes 393224 | tf_op jit(solution)/shard_map/ppermute | solution.py:25
  7.4 2.1 %collective-permute-start.1 = (bf16[512,128]{1,0:T(8,128)(2,1)S(1)}, bf16[512,128]{1,0:T(8,128)(2,1)S(1)}, u32[]{:S(2)}, u32[]{:S(2)}) collective-permute-start(bf16[512,128]{1,0:T(8,128)(2,1)S(1)} %bitcast.14), channel_id=1, source_target_pairs={{8,0},{16,8},{24,16},{0,24},{9,1},{17,9},{25,17},{1,25},{10,2},{18... | collective-permute-start | bytes 393224 | tf_op jit(solution)/shard_map/ppermute | solution.py:26
  9.5 0.0 copy-done.2
  9.5 0.1 reshape.36.v_ref
  9.6 0.0 copy-start.1
  9.6 0.6 %copy-done.1 = s32[1,1,1,7,1]{3,4,2,1,0:T(1,128)S(1)} copy-done((s32[1,1,1,7,1]{3,4,2,1,0:T(1,128)S(1)}, s32[1,1,1,7,1]{3,4,2,1,0:T(1,128)}, u32[]{:S(2)}) %copy-start.1) | copy-done | bytes 52
  10.3 1.8 %own_cells.1 = (bf16[128,2048]{1,0:T(8,128)(2,1)S(1)}, bf16[128,128]{1,0:T(8,128)(2,1)S(1)}, bf16[128,128]{1,0:T(8,128)(2,1)S(1)}, s32[7,8,128]{2,1,0:T(8,128)S(1)}) custom-call(bf16[2048,128]{1,0:T(8,128)(2,1)S(1)} %bitcast.10, f32[1,2048]{1,0:T(1,128)S(1)} %reshape.36.v_ref, s32[7]{0:T(128)S(1)} %bitcast.11, s32[1]{0:T(128)} %bitcast.me_ref), custom_call_target="tpu_custom_call" | custom-call | flops 2000000000 | bytes 524288 | tf_op jit(solution)/shard_map/own_cells/pallas_call | solution.py:170
  12.0 0.0 collective-permute-done.4
  12.1 0.0 collective-permute-done.2.yl
  12.1 0.0 collective-permute-done.3.yh
  12.1 0.4 %lateral_faces.1.early_ref = bf16[8,128,128]{2,1,0:T(8,128)(2,1)S(1)} custom-call(bf16[128,2048]{1,0:T(8,128)(2,1)S(1)} %get-tuple-element.9.lt_ref, bf16[128,128]{1,0:T(8,128)(2,1)S(1)} %get-tuple-element.12.dev_ref, bf16[128,128]{1,0:T(8,128)(2,1)S(1)} %get-tuple-element.10.ham_ref, s32[7,8,128]{2,1,0:T(8,128)S(1)} %get-tuple-element.11.slot_ref, ...), custom_call_target="tpu_custom_call" | custom-call | flops 500000000 | bytes 262144 | tf_op jit(solution)/shard_map/lateral_faces/pallas_call | solution.py:196
  12.5 1.3 %collective-permute-done.xl = bf16[512,128]{1,0:T(8,128)(2,1)S(1)} collective-permute-done((bf16[512,128]{1,0:T(8,128)(2,1)S(1)}, bf16[512,128]{1,0:T(8,128)(2,1)S(1)}, u32[]{:S(2)}, u32[]{:S(2)}) %collective-permute-start) | collective-permute-done | bytes 131104 | tf_op jit(solution)/shard_map/ppermute | solution.py:25
  13.8 1.5 %collective-permute-done.1.xh = bf16[512,128]{1,0:T(8,128)(2,1)S(1)} collective-permute-done((bf16[512,128]{1,0:T(8,128)(2,1)S(1)}, bf16[512,128]{1,0:T(8,128)(2,1)S(1)}, u32[]{:S(2)}, u32[]{:S(2)}) %collective-permute-start.1) | collective-permute-done | bytes 131104 | tf_op jit(solution)/shard_map/ppermute | solution.py:26
  15.3 0.4 %first_faces.1 = bf16[8,128,128]{2,1,0:T(8,128)(2,1)S(1)} custom-call(bf16[128,2048]{1,0:T(8,128)(2,1)S(1)} %get-tuple-element.9.lt_ref, bf16[128,128]{1,0:T(8,128)(2,1)S(1)} %get-tuple-element.10.ham_ref, s32[7,8,128]{2,1,0:T(8,128)S(1)} %get-tuple-element.11.slot_ref, bf16[512,128]{1,0:T(8,128)(2,1)S(1)} %collective-permute-done.xl, ...), custom_call_target="tpu_custom_call" | custom-call | flops 500000000 | bytes 262144 | tf_op jit(solution)/shard_map/first_faces/pallas_call | solution.py:205
  15.7 1.2 %collective-permute-start.5 = (bf16[2,128,128]{2,1,0:T(8,128)(2,1)S(1)}, bf16[2,128,128]{2,1,0:T(8,128)(2,1)S(1)}, u32[]{:S(2)}, u32[]{:S(2)}) collective-permute-start(bf16[2,128,128]{2,1,0:T(8,128)(2,1)S(1)} %get-tuple-element.21), channel_id=1, source_target_pairs={{0,8},{8,16},{16,24},{24,0},{1,9},{9,17},{17,25},{25,1},{2,10},{10... | collective-permute-start | bytes 196616 | tf_op jit(solution)/shard_map/ppermute | solution.py:218
  16.9 1.7 %collective-permute-start.6 = (bf16[2,128,128]{2,1,0:T(8,128)(2,1)S(1)}, bf16[2,128,128]{2,1,0:T(8,128)(2,1)S(1)}, u32[]{:S(2)}, u32[]{:S(2)}) collective-permute-start(bf16[2,128,128]{2,1,0:T(8,128)(2,1)S(1)} %get-tuple-element.20), channel_id=1, source_target_pairs={{0,16},{8,24},{16,0},{24,8},{1,17},{9,25},{17,1},{25,9},{2,18},{10... | collective-permute-start | bytes 196616 | tf_op jit(solution)/shard_map/ppermute | solution.py:218
  18.6 1.3 %collective-permute-start.7 = (bf16[2,128,128]{2,1,0:T(8,128)(2,1)S(1)}, bf16[2,128,128]{2,1,0:T(8,128)(2,1)S(1)}, u32[]{:S(2)}, u32[]{:S(2)}) collective-permute-start(bf16[2,128,128]{2,1,0:T(8,128)(2,1)S(1)} %get-tuple-element.19), channel_id=1, source_target_pairs={{0,24},{8,0},{16,8},{24,16},{1,25},{9,1},{17,9},{25,17},{2,26},{10... | collective-permute-start | bytes 196616 | tf_op jit(solution)/shard_map/ppermute | solution.py:218
  20.0 2.4 %collective-permute-done.5.refs_1_ = bf16[2,128,128]{2,1,0:T(8,128)(2,1)S(1)} collective-permute-done((bf16[2,128,128]{2,1,0:T(8,128)(2,1)S(1)}, bf16[2,128,128]{2,1,0:T(8,128)(2,1)S(1)}, u32[]{:S(2)}, u32[]{:S(2)}) %collective-permute-start.5) | collective-permute-done | bytes 65568 | tf_op jit(solution)/shard_map/ppermute | solution.py:218
  22.3 1.6 %collective-permute-done.6.refs_2_ = bf16[2,128,128]{2,1,0:T(8,128)(2,1)S(1)} collective-permute-done((bf16[2,128,128]{2,1,0:T(8,128)(2,1)S(1)}, bf16[2,128,128]{2,1,0:T(8,128)(2,1)S(1)}, u32[]{:S(2)}, u32[]{:S(2)}) %collective-permute-start.6) | collective-permute-done | bytes 65568 | tf_op jit(solution)/shard_map/ppermute | solution.py:218
  24.0 0.0 collective-permute-done.7.refs_3_
  24.0 0.7 %gather_slots.1 = bf16[8,128,128]{2,1,0:T(8,128)(2,1)} custom-call(s32[1]{0:T(128)} %bitcast.me_ref, bf16[2,128,128]{2,1,0:T(8,128)(2,1)S(1)} %get-tuple-element.22.refs_0_, bf16[2,128,128]{2,1,0:T(8,128)(2,1)S(1)} %collective-permute-done.5.refs_1_, bf16[2,128,128]{2,1,0:T(8,128)(2,1)S(1)} %collective-permute-done.6.refs_2_, ...), custom_call_target="tpu_custom_call" | custom-call | tf_op jit(solution)/shard_map/gather_slots/pallas_call | solution.py:231
  (5 shorter events, 0.1 us)
Async XLA Ops:
  0.0 1.8 %copy-start = (bf16[8,16,16,128]{3,2,1,0:T(8,128)(2,1)S(1)}, bf16[8,16,16,128]{3,2,1,0:T(8,128)(2,1)}, u32[]{:S(2)}) copy-start(bf16[8,16,16,128]{3,2,1,0:T(8,128)(2,1)} %param.3) | copy-start | bytes 1572868
  1.2 10.8 %collective-permute-start.4 = (bf16[512,128]{1,0:T(8,128)(2,1)S(1)}, bf16[512,128]{1,0:T(8,128)(2,1)S(1)}, u32[]{:S(2)}, u32[]{:S(2)}) collective-permute-start(bf16[512,128]{1,0:T(8,128)(2,1)S(1)} %pad_maximum_fusion), channel_id=1, source_target_pairs={{0,1},{1,0},{2,3},{3,2},{4,5},{5,4},{6,7},{7,6},{8,9},{9,8},{10,11... | collective-permute-start | bytes 393224 | tf_op jit(solution)/shard_map/ppermute | solution.py:23
  1.8 10.3 %collective-permute-start.2 = (bf16[256,128]{1,0:T(8,128)(2,1)S(1)}, bf16[256,128]{1,0:T(8,128)(2,1)S(1)}, u32[]{:S(2)}, u32[]{:S(2)}) collective-permute-start(bf16[256,128]{1,0:T(8,128)(2,1)S(1)} %bitcast.17), channel_id=1, source_target_pairs={{0,2},{2,4},{4,6},{6,0},{1,3},{3,5},{5,7},{7,1},{8,10},{10,12},{12... | collective-permute-start | bytes 196616 | tf_op jit(solution)/shard_map/ppermute | solution.py:25
  4.3 5.2 %copy-start.2 = (f32[8,16,16]{2,1,0:T(8,128)S(1)}, f32[8,16,16]{2,1,0:T(8,128)}, u32[]{:S(2)}) copy-start(f32[8,16,16]{2,1,0:T(8,128)} %param.4) | copy-start | bytes 24580
  4.3 7.7 %collective-permute-start.3 = (bf16[256,128]{1,0:T(8,128)(2,1)S(1)}, bf16[256,128]{1,0:T(8,128)(2,1)S(1)}, u32[]{:S(2)}, u32[]{:S(2)}) collective-permute-start(bf16[256,128]{1,0:T(8,128)(2,1)S(1)} %bitcast.16), channel_id=1, source_target_pairs={{2,0},{4,2},{6,4},{0,6},{3,1},{5,3},{7,5},{1,7},{10,8},{12,10},{14... | collective-permute-start | bytes 196616 | tf_op jit(solution)/shard_map/ppermute | solution.py:26
  5.4 8.4 %collective-permute-start = (bf16[512,128]{1,0:T(8,128)(2,1)S(1)}, bf16[512,128]{1,0:T(8,128)(2,1)S(1)}, u32[]{:S(2)}, u32[]{:S(2)}) collective-permute-start(bf16[512,128]{1,0:T(8,128)(2,1)S(1)} %bitcast.15), channel_id=1, source_target_pairs={{0,8},{8,16},{16,24},{24,0},{1,9},{9,17},{17,25},{25,1},{2,10},{10... | collective-permute-start | bytes 393224 | tf_op jit(solution)/shard_map/ppermute | solution.py:25
  7.4 7.9 %collective-permute-start.1 = (bf16[512,128]{1,0:T(8,128)(2,1)S(1)}, bf16[512,128]{1,0:T(8,128)(2,1)S(1)}, u32[]{:S(2)}, u32[]{:S(2)}) collective-permute-start(bf16[512,128]{1,0:T(8,128)(2,1)S(1)} %bitcast.14), channel_id=1, source_target_pairs={{8,0},{16,8},{24,16},{0,24},{9,1},{17,9},{25,17},{1,25},{10,2},{18... | collective-permute-start | bytes 393224 | tf_op jit(solution)/shard_map/ppermute | solution.py:26
  9.6 0.7 %copy-start.1 = (s32[1,1,1,7,1]{3,4,2,1,0:T(1,128)S(1)}, s32[1,1,1,7,1]{3,4,2,1,0:T(1,128)}, u32[]{:S(2)}) copy-start(s32[1,1,1,7,1]{3,4,2,1,0:T(1,128)} %param.5) | copy-start | bytes 88
  15.7 6.6 %collective-permute-start.5 = (bf16[2,128,128]{2,1,0:T(8,128)(2,1)S(1)}, bf16[2,128,128]{2,1,0:T(8,128)(2,1)S(1)}, u32[]{:S(2)}, u32[]{:S(2)}) collective-permute-start(bf16[2,128,128]{2,1,0:T(8,128)(2,1)S(1)} %get-tuple-element.21), channel_id=1, source_target_pairs={{0,8},{8,16},{16,24},{24,0},{1,9},{9,17},{17,25},{25,1},{2,10},{10... | collective-permute-start | bytes 196616 | tf_op jit(solution)/shard_map/ppermute | solution.py:218
  16.9 7.1 %collective-permute-start.6 = (bf16[2,128,128]{2,1,0:T(8,128)(2,1)S(1)}, bf16[2,128,128]{2,1,0:T(8,128)(2,1)S(1)}, u32[]{:S(2)}, u32[]{:S(2)}) collective-permute-start(bf16[2,128,128]{2,1,0:T(8,128)(2,1)S(1)} %get-tuple-element.20), channel_id=1, source_target_pairs={{0,16},{8,24},{16,0},{24,8},{1,17},{9,25},{17,1},{25,9},{2,18},{10... | collective-permute-start | bytes 196616 | tf_op jit(solution)/shard_map/ppermute | solution.py:218
  18.6 5.3 %collective-permute-start.7 = (bf16[2,128,128]{2,1,0:T(8,128)(2,1)S(1)}, bf16[2,128,128]{2,1,0:T(8,128)(2,1)S(1)}, u32[]{:S(2)}, u32[]{:S(2)}) collective-permute-start(bf16[2,128,128]{2,1,0:T(8,128)(2,1)S(1)} %get-tuple-element.19), channel_id=1, source_target_pairs={{0,24},{8,0},{16,8},{24,16},{1,25},{9,1},{17,9},{25,17},{2,26},{10... | collective-permute-start | bytes 196616 | tf_op jit(solution)/shard_map/ppermute | solution.py:218
